TPU v7x, 32 devices: a whole 2x2x4 slice. The times are simulated.
32 devices in a mesh: groups: 2 (over y), plane: 4 (over z), depth: 2 (over x), tok: 2 (over core).
Axes of the slice: x: 2, y: 2, z: 4, core: 2. Of those that a mesh axis runs over, the one named last changes fastest.
Arguments:
- tokens: bfloat16 [256, 2048], P(('groups', 'plane', 'depth', 'tok')), parts along dimension 0, may hold values from -6 to 6
- expert_ids: int32 [256, 4], P(('groups', 'plane', 'depth', 'tok')), parts along dimension 0, may hold values from 0 to 3, as said below
- slot_index: int32 [256, 4], P(('groups', 'plane', 'depth', 'tok')), parts along dimension 0, may hold values from 0 to 7, as said below
- route_weight: bfloat16 [256, 4], P(('groups', 'plane', 'depth', 'tok')), parts along dimension 0, may hold values from 0.099609375 to 1
- shared_gate: bfloat16 [2048], replicated, may hold values from -0.125 to 0.125
- shared_gate_up: bfloat16 [2, 2048, 5632], P(None, None, 'plane'), may hold values from -0.125 to 0.125
- shared_down: bfloat16 [5632, 2048], P('plane'), may hold values from -0.078125 to 0.078125
- expert_gate_up: bfloat16 [4, 2, 2048, 1408], P('plane', None, None, ('depth', 'tok')), may hold values from -0.125 to 0.125
- expert_down: bfloat16 [4, 1408, 2048], P('plane', ('depth', 'tok')), may hold values from -0.15625 to 0.15625
Outputs:
- mixed: bfloat16 [256, 2048], P(('groups', 'plane', 'depth', 'tok')), parts along dimension 0
There are 2 independent parts, one for each index of `groups`. A program takes and returns all parts, laid end to end along the dimension named above; an argument that names none is the same for every part. Nothing has to cross between parts.
Inputs may be any that keep to these rules, and one draw needn't show every extreme that they name: `expert_ids`: each row names 4 different experts. Among the choices of the rows of one device that name the same expert, slot_index takes each value from 0 to their count minus one exactly once, in an order that varies from draw to draw; the capacity 8 is filled on some devices.
All inputs are finite; a program needn't handle non-finite values.
Results may differ from a plain program's by a relative error of at most 0.019.
Values may be sent and summed in bfloat16 or wider, within the bound.
A program may use at most 64 MiB of HBM per device.

v0:
```python
import jax
import jax.numpy as jnp
from jax import lax
from jax.sharding import PartitionSpec as P


def gated_rows(token_rows, gate_up):
    gate_part = jnp.dot(token_rows, gate_up[0], preferred_element_type=jnp.float32)
    up_part = jnp.dot(token_rows, gate_up[1], preferred_element_type=jnp.float32)
    return (jax.nn.silu(gate_part) * up_part).astype(jnp.bfloat16)


def expert_rows(received, gate_up, down_proj):
    hidden = gated_rows(lax.all_gather(received, ("depth", "tok"), axis=0, tiled=True), gate_up)
    return lax.psum_scatter(
        jnp.dot(hidden, down_proj, preferred_element_type=jnp.float32).astype(jnp.bfloat16),
        ("depth", "tok"),
        scatter_dimension=0,
        tiled=True,
    ).astype(jnp.float32)


def on_device(
    tokens,
    expert_ids,
    slot_index,
    route_weight,
    shared_gate,
    shared_gate_up,
    shared_down,
    expert_gate_up,
    expert_down,
):
    planes = lax.axis_size("plane")
    tok_rows = tokens.shape[0]
    choose_count = expert_ids.shape[1]
    model_width = tokens.shape[1]
    capacity = max(2, tok_rows * choose_count // planes)
    slot_total = planes * capacity
    local_gate_up = expert_gate_up[0]
    local_down = expert_down[0]
    column = lax.broadcasted_iota(jnp.int32, (slot_total, 1, 1), 0)
    kept_mask = slot_index < capacity
    target = jnp.where(kept_mask, expert_ids * capacity + slot_index, -1)
    matches = target[None, :, :] == column
    spread = jnp.any(matches, axis=2).astype(jnp.bfloat16)
    outgoing = jnp.dot(spread, tokens, preferred_element_type=jnp.float32).astype(jnp.bfloat16)
    outgoing = outgoing.reshape(planes, capacity, model_width)
    routed_slots = lax.all_to_all(
        expert_rows(
            lax.all_to_all(outgoing, "plane", split_axis=0, concat_axis=0, tiled=True),
            local_gate_up,
            local_down,
        ).astype(jnp.bfloat16),
        "plane",
        split_axis=0,
        concat_axis=0,
        tiled=True,
    ).astype(jnp.float32)
    weights = route_weight.astype(jnp.float32)
    combine = jnp.sum(jnp.where(matches, weights[None, :, :], 0.0), axis=2).T
    routed = jnp.dot(
        combine,
        routed_slots.reshape(slot_total, model_width),
        precision=lax.Precision.HIGHEST,
        preferred_element_type=jnp.float32,
    )
    shared_hidden = gated_rows(lax.all_gather(tokens, "plane", axis=0, tiled=True), shared_gate_up)
    shared_out = lax.psum_scatter(
        jnp.dot(shared_hidden, shared_down, preferred_element_type=jnp.float32).astype(
            jnp.bfloat16
        ),
        "plane",
        scatter_dimension=0,
        tiled=True,
    ).astype(jnp.float32)
    shared_scale = jax.nn.sigmoid(jnp.dot(tokens, shared_gate, preferred_element_type=jnp.float32))
    result = shared_scale[:, None] * shared_out + routed
    return result.astype(jnp.bfloat16)


def solution(mesh):
    in_specs = (
        P(("groups", "plane", "depth", "tok"), None),
        P(("groups", "plane", "depth", "tok"), None),
        P(("groups", "plane", "depth", "tok"), None),
        P(("groups", "plane", "depth", "tok"), None),
        P(),
        P(None, None, "plane"),
        P("plane", None),
        P("plane", None, None, ("depth", "tok")),
        P("plane", ("depth", "tok"), None),
    )
    out_specs = P(("groups", "plane", "depth", "tok"), None)
    return jax.shard_map(
        on_device, mesh=mesh, in_specs=in_specs, out_specs=out_specs, check_vma=False
    )
```

profile of v0, /device:TPU:0, one launch (start us, length us, event | category | flops | bytes accessed | tf_op | source)
XLA Modules:
  0.0 94.5 jit_solution(18416283824460108339)
XLA Ops:
  6.5 0.0 copy-start
  6.5 0.8 add_select_fusion
  7.4 0.1 fusion.48
  7.4 1.6 %fusion.12 = bf16[4,8,2048]{2,1,0:T(8,128)(2,1)} fusion(pred[32,8]{0,1:T(8,128)(4,1)S(1)} %fusion.48, bf16[8,2048]{1,0:T(8,128)(2,1)} %param.9), kind=kOutput, calls=%fused_computation.11 | convolution fusion | flops 1114112 | bytes 164096 | tf_op jit(solution)/shard_map/dot_general | solution.py:47
  9.1 6.3 %all-to-all-start = ((bf16[4,8,2048]{2,1,0:T(8,128)(2,1)}), bf16[4,8,2048]{2,1,0:T(8,128)(2,1)S(1)}, u32[]{:S(2)}, u32[]{:S(2)}) async-start(bf16[4,8,2048]{2,1,0:T(8,128)(2,1)} %fusion.12), calls=%async_computation.1 | async-start | bytes 262144 | tf_op jit(solution)/shard_map/all_to_all | solution.py:51
  15.4 0.0 reduce-scatter.5.cloned.1.call-start
  15.4 14.1 %all_gather.6 = bf16[32,2048]{1,0:T(8,128)(2,1)S(1)} all-gather(bf16[8,2048]{1,0:T(8,128)(2,1)} %param.9), channel_id=1, replica_groups=mesh['groups'=2,'plane'=4,'depth'=2,'tok'=2] {'plane'}, dimensions={0}, use_global_device_ids=true | all-gather | bytes 163840 | tf_op jit(solution)/shard_map/all_gather | solution.py:68
  29.6 0.0 all-to-all-done
  29.6 7.2 %all_gather.7 = bf16[16,8,2048]{2,1,0:T(8,128)(2,1)S(1)} all-gather(bf16[4,8,2048]{2,1,0:T(8,128)(2,1)S(1)} %all-to-all-done), channel_id=1, replica_groups=mesh['groups'=2,'plane'=4,'depth'=2,'tok'=2] {'depth','tok'}, dimensions={0}, use_global_device_ids=true | all-gather | bytes 655360 | tf_op jit(solution)/shard_map/all_gather | solution.py:14
  36.7 2.0 %fusion.16 = f32[16,8,352]{2,1,0:T(8,128)S(1)} fusion(bf16[16,8,2048]{2,1,0:T(8,128)(2,1)S(1)} %all_gather.7, bf16[1,2,2048,352]{2,3,1,0:T(8,128)(2,1)} %param.16), kind=kOutput, calls=%fused_computation.16 | convolution fusion | flops 184549376 | bytes 2146304 | tf_op jit(solution)/shard_map/dot_general | solution.py:8
  38.7 0.0 copy-done
  38.7 3.4 %convolution_convert_fusion = bf16[16,8,2048]{2,1,0:T(8,128)(2,1)} fusion(bf16[1,352,2048]{2,1,0:T(8,128)(2,1)S(1)} %copy-done, bf16[16,8,2048]{2,1,0:T(8,128)(2,1)S(1)} %all_gather.7, bf16[1,2,2048,352]{2,3,1,0:T(8,128)(2,1)} %param.16, f32[16,8,352]{2,1,0:T(8,128)S(1)} %fusion.16), kind=kOutput, calls=%fused_computation.6 | convolution fusion | flops 369631232 | bytes 4112384 | tf_op jit(solution)/shard_map/dot_general | solution.py:16
  42.1 0.0 reduce-scatter.5.cloned.1.call-update
  42.1 0.0 reduce-scatter.3.cloned.1.call-start
  42.2 3.7 %fusion.2 = f32[32,1408]{1,0:T(8,128)S(1)} fusion(bf16[32,2048]{1,0:T(8,128)(2,1)S(1)} %all_gather.6, bf16[2,2048,1408]{2,1,0:T(8,128)(2,1)} %param.14), kind=kOutput, calls=%fused_computation.2 | convolution fusion | flops 184549376 | bytes 6078464 | tf_op jit(solution)/shard_map/dot_general | solution.py:8
  45.8 0.0 copy-start.3
  45.8 0.0 copy-start.2
  45.9 0.0 copy-start.1
  45.9 7.2 %convolution_convert_fusion.2 = bf16[32,2048]{1,0:T(8,128)(2,1)} fusion(bf16[1408,2048]{1,0:T(8,128)(2,1)} %param.15, bf16[32,2048]{1,0:T(8,128)(2,1)S(1)} %all_gather.6, bf16[2,2048,1408]{2,1,0:T(8,128)(2,1)} %param.14, f32[32,1408]{1,0:T(8,128)S(1)} %fusion.2), kind=kOutput, calls=%fused_computation.10 | convolution fusion | flops 369434624 | bytes 11976704 | tf_op jit(solution)/shard_map/dot_general | solution.py:70
  53.1 0.0 reduce-scatter.3.cloned.1.call-update
  53.1 0.0 copy-done.3
  53.1 0.1 select_reduce_fusion
  53.2 0.0 copy-done.2
  53.2 11.1 %reduce-scatter.5.cloned.1.call-done = bf16[4,8,2048]{2,1,0:T(8,128)(2,1)} async-done(((bf16[16,8,2048]{2,1,0:T(8,128)(2,1)}), bf16[4,8,2048]{2,1,0:T(8,128)(2,1)}) %reduce-scatter.5.cloned.1.call-update) | async-done | bytes 131088 | tf_op jit(solution)/shard_map/reduce_scatter | solution.py:15
  64.3 4.6 %all-to-all-start.1 = ((bf16[4,8,2048]{2,1,0:T(8,128)(2,1)}), bf16[4,8,2048]{2,1,0:T(8,128)(2,1)S(1)}, u32[]{:S(2)}, u32[]{:S(2)}) async-start(bf16[4,8,2048]{2,1,0:T(8,128)(2,1)} %reduce-scatter.5.cloned.1.call-done), calls=%async_computation.3 | async-start | bytes 262144 | tf_op jit(solution)/shard_map/all_to_all | solution.py:49
  68.9 0.0 copy-done.1
  69.0 0.1 fusion.32
  69.1 17.0 %reduce-scatter.3.cloned.1.call-done = bf16[8,2048]{1,0:T(8,128)(2,1)} async-done(((bf16[32,2048]{1,0:T(8,128)(2,1)}), bf16[8,2048]{1,0:T(8,128)(2,1)}) %reduce-scatter.3.cloned.1.call-update) | async-done | bytes 32784 | tf_op jit(solution)/shard_map/reduce_scatter | solution.py:69
  86.1 0.0 all-to-all-done.1
  86.1 1.5 %fusion.13 = bf16[8,2048]{1,0:T(8,128)(2,1)} fusion(f32[32,8]{0,1:T(8,128)S(1)} %select_reduce_fusion, bf16[4,8,2048]{2,1,0:T(8,128)(2,1)S(1)} %all-to-all-done.1, bf16[8,2048]{1,0:T(8,128)(2,1)} %reduce-scatter.3.cloned.1.call-done, f32[8]{0:T(128)S(1)} %fusion.32), kind=kOutput, calls=%fused_computation.13 | convolution fusion | flops 6356992 | bytes 197664 | tf_op jit(solution)/shard_map/dot_general | solution.py:62
  (2 shorter events, 0.0 us)
Async XLA Ops:
  6.5 32.2 %copy-start = (bf16[1,352,2048]{2,1,0:T(8,128)(2,1)S(1)}, bf16[1,352,2048]{2,1,0:T(8,128)(2,1)}, u32[]{:S(2)}) copy-start(bf16[1,352,2048]{2,1,0:T(8,128)(2,1)} %param.17) | copy-start | bytes 4325380
  9.1 20.5 %all-to-all-start = ((bf16[4,8,2048]{2,1,0:T(8,128)(2,1)}), bf16[4,8,2048]{2,1,0:T(8,128)(2,1)S(1)}, u32[]{:S(2)}, u32[]{:S(2)}) async-start(bf16[4,8,2048]{2,1,0:T(8,128)(2,1)} %fusion.12), calls=%async_computation.1 | async-start | bytes 262144 | tf_op jit(solution)/shard_map/all_to_all | solution.py:51
  15.4 48.9 %reduce-scatter.5.cloned.1.call-start = ((), (), s32[]{:S(2)}) async-start(), calls=%async_computation.5 | async-start | bytes 655360 | tf_op jit(solution)/shard_map/reduce_scatter | solution.py:15
  42.1 44.0 %reduce-scatter.3.cloned.1.call-start = ((), (), s32[]{:S(2)}) async-start(), calls=%async_computation.4 | async-start | bytes 163840 | tf_op jit(solution)/shard_map/reduce_scatter | solution.py:69
  45.8 7.3 %copy-start.3 = (bf16[8,4]{0,1:T(4,128)(2,1)S(1)}, bf16[8,4]{0,1:T(4,128)(2,1)}, u32[]{:S(2)}) copy-start(bf16[8,4]{0,1:T(4,128)(2,1)} %param.12) | copy-start | bytes 196
  45.8 7.4 %copy-start.2 = (bf16[2048]{0:T(1024)(128)(2,1)S(1)}, bf16[2048]{0:T(1024)(128)(2,1)}, u32[]{:S(2)}) copy-start(bf16[2048]{0:T(1024)(128)(2,1)} %param.13) | copy-start | bytes 12292
  45.9 23.1 %copy-start.1 = (bf16[8,2048]{1,0:T(8,128)(2,1)S(1)}, bf16[8,2048]{1,0:T(8,128)(2,1)}, u32[]{:S(2)}) copy-start(bf16[8,2048]{1,0:T(8,128)(2,1)} %param.9) | copy-start | bytes 98308
  64.3 21.7 %all-to-all-start.1 = ((bf16[4,8,2048]{2,1,0:T(8,128)(2,1)}), bf16[4,8,2048]{2,1,0:T(8,128)(2,1)S(1)}, u32[]{:S(2)}, u32[]{:S(2)}) async-start(bf16[4,8,2048]{2,1,0:T(8,128)(2,1)} %reduce-scatter.5.cloned.1.call-done), calls=%async_computation.3 | async-start | bytes 262144 | tf_op jit(solution)/shard_map/all_to_all | solution.py:49
Sparse Core Ops, SparseCore 0:
  42.2 22.0 reduce-scatter.4
  66.6 19.4 reduce-scatter.2
where the time goes:
time: 95 us; the launch traced here: 94.5 us
  waiting for transfers between devices  28.1 us (30%)
  blocking collectives  21.3 us (22%)
  matrix products  19.5 us (21%)
  between operations  13.5 us (14%)
  starting transfers between devices  11 us (12%)
  other arithmetic  0.97 us (1%)
    reduce_scatter x1, waiting for transfers between devices, on_device(): lax.psum_scatter(jnp.dot(shared_hidden, shared_down, preferred_element_ty...  17 us
    all_gather x1, blocking collectives, on_device(): lax.all_gather(tokens, 'plane', axis=0, tiled=True)  14.1 us
    reduce_scatter x1, waiting for transfers between devices, expert_rows(): lax.psum_scatter(jnp.dot(hidden, down_proj, preferred_element_type=jnp.fl...  11.1 us
    dot_general x1, matrix products, on_device(): jnp.dot(shared_hidden, shared_down, preferred_element_type=jnp.float32)  7.22 us
    all_gather x1, blocking collectives, expert_rows(): lax.all_gather(received, ('depth', 'tok'), axis=0, tiled=True)  7.16 us
    all_to_all x1, starting transfers between devices, on_device(): lax.all_to_all(outgoing, 'plane', split_axis=0, concat_axis=0, tiled=True)  6.35 us
    dot_general x2, matrix products, gated_rows(): jnp.dot(token_rows, gate_up[0], preferred_element_type=jnp.float32)  5.62 us
    all_to_all x1, starting transfers between devices, on_device(): lax.all_to_all(expert_rows(lax.all_to_all(outgoing, 'plane', split_axis=0...  4.6 us
  transfers between devices with their start and end apart: 4, of which 2 were waited for; matrix products, arithmetic and copies ran while one was open for 12% of the time, Pallas kernels for 0%

commit v1 on v0

--- a/solution.py
+++ b/solution.py
@@ -1,6 +1,10 @@
+import functools
+
 import jax
 import jax.numpy as jnp
 from jax import lax
+from jax.experimental import pallas as pl
+from jax.experimental.pallas import tpu as pltpu
 from jax.sharding import PartitionSpec as P
 
 
@@ -79,6 +83,284 @@
     return result.astype(jnp.bfloat16)
 
 
+LANES = 128
+COLUMN_CHUNKS = 4
+MESH = pl.DeviceIdType.MESH
+
+
+def planes_by_distance(me, planes):
+    orders = [sorted((q for q in range(planes) if q != p), key=lambda q: abs(q - p)) for p in range(planes)]
+    picked = []
+    for place in range(planes - 1):
+        value = jnp.int32(orders[0][place])
+        for p in range(1, planes):
+            value = jnp.where(me == p, jnp.int32(orders[p][place]), value)
+        picked.append(value)
+    return picked
+
+
+def block_kernel(
+    planes,
+    tok_hbm,
+    ids_hbm,
+    slot_hbm,
+    rw_hbm,
+    sg_ref,
+    sgu_hbm,
+    sdn_hbm,
+    egu_hbm,
+    edn_hbm,
+    out_ref,
+    xb,
+    ids_v,
+    slot_v,
+    rw_v,
+    sgu_v,
+    sdn_v,
+    egu_v,
+    edn_v,
+    keep,
+    st,
+    rt,
+    sx,
+    rx,
+    vkeep,
+    sz,
+    rz,
+    local_sem,
+    ag_send,
+    ag_recv,
+    t_send,
+    t_recv,
+    x_send,
+    x_recv,
+    z_send,
+    z_recv,
+):
+    p = lax.axis_index("plane")
+    d = lax.axis_index("depth")
+    t = lax.axis_index("tok")
+    rows, width = tok_hbm.shape
+    choices = ids_hbm.shape[1]
+    shared_units = sdn_hbm.shape[0]
+    panel = sdn_v.shape[0]
+    chunks = st.shape[0]
+    span = width // chunks
+    half = st.shape[1]
+    quarter = half // 2
+    near = planes_by_distance(p, planes)
+    to_x = {"depth": 1 - d}
+    to_t = {"tok": 1 - t}
+
+    shard = d * 2 + t
+    start = pl.multiple_of(jnp.minimum(shard * panel, shared_units - panel), LANES)
+
+    def local(src, dst, index):
+        copy = pltpu.make_async_copy(src, dst, local_sem.at[index])
+        copy.start()
+        return copy
+
+    tok_copy = local(tok_hbm, xb.at[p, :, pl.ds(0, width)], 0)
+    small = [
+        local(ids_hbm, ids_v, 1),
+        local(slot_hbm, slot_v, 2),
+        local(rw_hbm, rw_v, 3),
+    ]
+    barrier = pltpu.get_barrier_semaphore()
+    for peer in [{"plane": q} for q in near] + [to_x, to_t]:
+        pl.semaphore_signal(barrier, inc=1, device_id=peer, device_id_type=MESH)
+    up_copies = [
+        local(egu_hbm.at[0], egu_v, 4),
+        local(sgu_hbm.at[:, :, pl.ds(start, panel)], sgu_v, 5),
+    ]
+    down_copies = [
+        local(edn_hbm.at[0], edn_v, 6),
+        local(sdn_hbm.at[pl.ds(start, panel), :], sdn_v, 7),
+    ]
+
+    for copy in small:
+        copy.wait()
+    lane = lax.broadcasted_iota(jnp.int32, (rows, LANES), 1)
+    ids = ids_v[...]
+    slots = slot_v[...]
+    weights = rw_v[...].astype(jnp.float32)
+    capacity = max(2, rows * choices // planes)
+    share = jnp.zeros((rows, LANES), jnp.float32)
+    for k in range(choices):
+        hit = (ids[:, k : k + 1] == lane) & (slots[:, k : k + 1] < capacity)
+        share = share + jnp.where(hit, weights[:, k : k + 1], 0.0)
+    xb[p, :, width:] = share.astype(jnp.bfloat16)
+    tok_copy.wait()
+    pl.semaphore_wait(barrier, planes + 1)
+
+    def block(rel_t, rel_d, q):
+        return xb.at[(rel_t * 2 + rel_d) * planes + q]
+
+    pending = []
+
+    def remote(src, dst, send_sem, recv_sem, device):
+        copy = pltpu.make_async_remote_copy(
+            src_ref=src,
+            dst_ref=dst,
+            send_sem=send_sem,
+            recv_sem=recv_sem,
+            device_id=device,
+            device_id_type=MESH,
+        )
+        copy.start()
+        pending.append(copy)
+
+    def landed(dst, send_sem, recv_sem):
+        pltpu.make_async_remote_copy(
+            src_ref=dst,
+            dst_ref=dst,
+            send_sem=send_sem,
+            recv_sem=recv_sem,
+            device_id=to_t,
+            device_id_type=MESH,
+        ).wait_recv()
+
+    for q in reversed(near):
+        remote(block(0, 0, p), block(0, 0, p), ag_send.at[0, q], ag_recv.at[0, p], {"plane": q})
+
+    def pass_x(q):
+        remote(block(0, 0, q), block(0, 1, q), ag_send.at[1, q], ag_recv.at[1, q], to_x)
+
+    def pass_t(rel_d, q):
+        remote(block(0, rel_d, q), block(1, rel_d, q), ag_send.at[2 + rel_d, q], ag_recv.at[2 + rel_d, q], to_t)
+
+    def from_z(q):
+        landed(block(0, 0, q), ag_send.at[0, q], ag_recv.at[0, q])
+        pass_x(q)
+        pass_t(0, q)
+
+    def from_x(q):
+        landed(block(0, 1, q), ag_send.at[1, q], ag_recv.at[1, q])
+        pass_t(1, q)
+
+    pass_x(p)
+    pass_t(0, p)
+    from_z(near[0])
+    from_x(p)
+    for place in range(1, planes - 1):
+        from_z(near[place])
+        from_x(near[place - 1])
+    from_x(near[-1])
+    for copy in up_copies:
+        copy.wait()
+    for rel_d in range(2):
+        for q in [p] + near:
+            landed(block(1, rel_d, q), ag_send.at[2 + rel_d, q], ag_recv.at[2 + rel_d, q])
+
+    total = xb.shape[0] * rows
+    x = xb[:, :, :width].reshape(total, width)
+
+    def gated(gate_up):
+        gate_part = jnp.dot(x, gate_up[0], preferred_element_type=jnp.float32)
+        up_part = jnp.dot(x, gate_up[1], preferred_element_type=jnp.float32)
+        return jax.nn.silu(gate_part) * up_part
+
+    expert_hidden = gated(egu_v).astype(jnp.bfloat16)
+    shared_hidden = gated(sgu_v)
+    unit = start + lax.broadcasted_iota(jnp.int32, shared_hidden.shape, 1)
+    shared_hidden = jnp.where(unit >= shard * panel, shared_hidden, 0.0).astype(jnp.bfloat16)
+    column = lax.broadcasted_iota(jnp.int32, (total, LANES), 1)
+    meta = xb[:, :, width:].reshape(total, LANES).astype(jnp.float32)
+    route = jnp.sum(jnp.where(column == p, meta, 0.0), axis=1, keepdims=True)
+    gate_rows = jnp.broadcast_to(sg_ref[...].reshape(1, width), (8, width))
+    score = lax.dot_general(x, gate_rows, (((1,), (1,)), ((), ())), preferred_element_type=jnp.float32)
+    scale = jax.nn.sigmoid(score[:, :1])
+
+    for copy in down_copies:
+        copy.wait()
+    for c in range(chunks):
+        cols = pl.ds(c * span, span)
+        part = route * jnp.dot(expert_hidden, edn_v[:, cols], preferred_element_type=jnp.float32)
+        part = part + scale * jnp.dot(shared_hidden, sdn_v[:, cols], preferred_element_type=jnp.float32)
+        st[c] = part[half:].astype(jnp.bfloat16)
+        remote(st.at[c], rt.at[c], t_send.at[c], t_recv.at[c], to_t)
+        keep[c] = part[:half]
+    for c in range(chunks):
+        landed(rt.at[c], t_send.at[c], t_recv.at[c])
+        sx[c] = (keep[c, quarter:] + rt[c, quarter:].astype(jnp.float32)).astype(jnp.bfloat16)
+        remote(sx.at[c], rx.at[c], x_send.at[c], x_recv.at[c], to_x)
+        keep[c, :quarter] = keep[c, :quarter] + rt[c, :quarter].astype(jnp.float32)
+    for c in range(chunks):
+        landed(rx.at[c], x_send.at[c], x_recv.at[c])
+        value = keep[c, :quarter] + rx[c].astype(jnp.float32)
+        value = value.reshape(planes, rows, span)
+        sz[c] = value.astype(jnp.bfloat16)
+        for q in reversed(near):
+            remote(sz.at[c, q], rz.at[c, p], z_send.at[c, q], z_recv.at[c, p], {"plane": q})
+        vkeep[c] = value
+    for c in range(chunks):
+        value = vkeep[c, p]
+        for q in near:
+            landed(rz.at[c, q], z_send.at[c, q], z_recv.at[c, q])
+            value = value + rz[c, q].astype(jnp.float32)
+        out_ref[:, c * span : (c + 1) * span] = value.astype(jnp.bfloat16)
+    for copy in pending:
+        copy.wait_send()
+
+
+def fused_block(planes, tokens, expert_ids, slot_index, route_weight, shared_gate, shared_gate_up, shared_down, expert_gate_up, expert_down):
+    rows, width = tokens.shape
+    units = shared_down.shape[0]
+    panel = -(-(units // LANES) // 4) * LANES
+    chunks = COLUMN_CHUNKS
+    span = width // chunks
+    bf16, f32 = jnp.bfloat16, jnp.float32
+    anywhere = pl.BlockSpec(memory_space=pl.ANY)
+    vmem = pl.BlockSpec(memory_space=pltpu.VMEM)
+    blocks = 4 * planes
+    return pl.pallas_call(
+        functools.partial(block_kernel, planes),
+        out_shape=jax.ShapeDtypeStruct((rows, width), bf16),
+        in_specs=[anywhere] * 4 + [vmem] + [anywhere] * 4,
+        out_specs=vmem,
+        scratch_shapes=[
+            pltpu.VMEM((blocks, rows, width + LANES), bf16),
+            pltpu.VMEM(expert_ids.shape, jnp.int32),
+            pltpu.VMEM(slot_index.shape, jnp.int32),
+            pltpu.VMEM(route_weight.shape, bf16),
+            pltpu.VMEM((2, width, panel), bf16),
+            pltpu.VMEM((panel, width), bf16),
+            pltpu.VMEM(expert_gate_up.shape[1:], bf16),
+            pltpu.VMEM(expert_down.shape[1:], bf16),
+            pltpu.VMEM((chunks, 2 * planes * rows, span), f32),
+            pltpu.VMEM((chunks, 2 * planes * rows, span), bf16),
+            pltpu.VMEM((chunks, 2 * planes * rows, span), bf16),
+            pltpu.VMEM((chunks, planes * rows, span), bf16),
+            pltpu.VMEM((chunks, planes * rows, span), bf16),
+            pltpu.VMEM((chunks, planes, rows, span), f32),
+            pltpu.VMEM((chunks, planes, rows, span), bf16),
+            pltpu.VMEM((chunks, planes, rows, span), bf16),
+            pltpu.SemaphoreType.DMA((8,)),
+            pltpu.SemaphoreType.DMA((4, planes)),
+            pltpu.SemaphoreType.DMA((4, planes)),
+            pltpu.SemaphoreType.DMA((chunks,)),
+            pltpu.SemaphoreType.DMA((chunks,)),
+            pltpu.SemaphoreType.DMA((chunks,)),
+            pltpu.SemaphoreType.DMA((chunks,)),
+            pltpu.SemaphoreType.DMA((chunks, planes)),
+            pltpu.SemaphoreType.DMA((chunks, planes)),
+        ],
+        compiler_params=pltpu.CompilerParams(collective_id=0, has_side_effects=True),
+        name="expert_block",
+    )(tokens, expert_ids, slot_index, route_weight, shared_gate.reshape(1, width), shared_gate_up, shared_down, expert_gate_up, expert_down)
+
+
+def on_any_device(mesh, tokens, expert_ids, slot_index, route_weight, shared_gate, shared_gate_up, shared_down, expert_gate_up, expert_down):
+    args = (tokens, expert_ids, slot_index, route_weight, shared_gate, shared_gate_up, shared_down, expert_gate_up, expert_down)
+    planes = mesh.shape["plane"]
+    every_expert = expert_ids.shape[1] == planes * expert_gate_up.shape[0] and expert_gate_up.shape[0] == 1
+    pairs = mesh.shape["depth"] == 2 and mesh.shape["tok"] == 2
+    tiled = tokens.shape[1] % (LANES * COLUMN_CHUNKS) == 0 and shared_down.shape[0] % LANES == 0
+    if every_expert and pairs and tiled:
+        return fused_block(planes, *args)
+    return on_device(*args)
+
+
 def solution(mesh):
     in_specs = (
         P(("groups", "plane", "depth", "tok"), None),
@@ -93,5 +375,5 @@
     )
     out_specs = P(("groups", "plane", "depth", "tok"), None)
     return jax.shard_map(
-        on_device, mesh=mesh, in_specs=in_specs, out_specs=out_specs, check_vma=False
+        functools.partial(on_any_device, mesh), mesh=mesh, in_specs=in_specs, out_specs=out_specs, check_vma=False
     )

time: 95 us -> 41.2 us (0.43)
  Pallas kernels: 0 us -> 29.5 us
  waiting for transfers between devices: 28.1 us -> 0 us
  blocking collectives: 21.3 us -> 0 us
  matrix products: 19.5 us -> 0 us
  between operations: 13.5 us -> 0.01 us
  local copies, waits for them, and re-layouts: 0.03 us -> 11.3 us
  starting transfers between devices: 11 us -> 0 us
  other arithmetic: 0.97 us -> 0 us
    pallas_call x0 -> x1, Pallas kernels: none -> 29.5 us  [fused_block(): pl.pallas_call(functools.partial(block_kernel, planes), out_shape=jax.Sha...]
    reduce_scatter x2 -> x0, waiting for transfers between devices: 28.1 us -> none  [the longest x1 17 us: on_device(): lax.psum_scatter(jnp.dot(shared_hidden, shared_down, preferred_element_ty...]
    all_gather x2 -> x0, blocking collectives: 21.3 us -> none  [the longest x1 14.1 us: on_device(): lax.all_gather(tokens, 'plane', axis=0, tiled=True)]
    dot_general x7 -> x0, matrix products: 19.5 us -> none  [the longest x1 7.22 us: on_device(): jnp.dot(shared_hidden, shared_down, preferred_element_type=jnp.float32)]
    all_to_all x2 -> x0, starting transfers between devices: 10.9 us -> none  [the longest x1 6.35 us: on_device(): lax.all_to_all(outgoing, 'plane', split_axis=0, concat_axis=0, tiled=True)]
    unnamed x9 -> x5, local copies, waits for them, and re-layouts: 0.03 us -> 10 us
    reshape x0 -> x1, local copies, waits for them, and re-layouts: none -> 1.29 us  [fused_block(): shared_gate.reshape(1, width)]
  transfers between devices with their start and end apart: 4 -> 0, of which waited for: 2 -> 0; matrix products, arithmetic and copies ran while one was open for 12% -> 0% of each run, Pallas kernels for 0% -> 0%
where the time goes in v1:
time: 41.2 us; the launch traced here: 40.8 us
  Pallas kernels  29.5 us (72%)
  local copies, waits for them, and re-layouts  11.3 us (27%)
    pallas_call x1, Pallas kernels, fused_block(): pl.pallas_call(functools.partial(block_kernel, planes), out_shape=jax.Sha...  29.5 us
    unnamed x5, local copies, waits for them, and re-layouts  10 us
    reshape x1, local copies, waits for them, and re-layouts, fused_block(): shared_gate.reshape(1, width)  1.29 us

profile of v1, /device:TPU:0, one launch (start us, length us, event | category | flops | bytes accessed | tf_op | source)
XLA Modules:
  0.0 40.8 jit_solution(12542195996742138735)
XLA Ops:
  0.0 1.4 %copy.12.rw_hbm = bf16[8,4]{1,0:T(8,128)(2,1)} copy(bf16[8,4]{0,1:T(4,128)(2,1)} %param.12) | data formatting | bytes 128 | tf_op args[3]
  1.4 1.3 %copy.10.ids_hbm = s32[8,4]{1,0:T(8,128)} copy(s32[8,4]{0,1:T(4,128)} %param.10) | data formatting | bytes 256 | tf_op args[1]
  2.7 1.3 %copy.11.slot_hbm = s32[8,4]{1,0:T(8,128)} copy(s32[8,4]{0,1:T(4,128)} %param.11) | data formatting | bytes 256 | tf_op args[2]
  4.0 1.3 %reshape.3.sg_ref = bf16[1,2048]{1,0:T(2,128)(2,1)} reshape(bf16[2048]{0:T(1024)(128)(2,1)} %param.13) | data formatting | bytes 8192 | tf_op jit(solution)/shard_map/reshape | solution.py:350
  5.3 4.6 %copy.13.egu_hbm = bf16[1,2,2048,352]{3,2,1,0:T(8,128)(2,1)} copy(bf16[1,2,2048,352]{2,3,1,0:T(8,128)(2,1)} %param.16) | data formatting | bytes 5767168 | tf_op args[7]
  9.9 29.5 %expert_block.1 = bf16[8,2048]{1,0:T(8,128)(2,1)} custom-call(bf16[8,2048]{1,0:T(8,128)(2,1)} %tok_hbm.1, s32[8,4]{1,0:T(8,128)} %copy.10.ids_hbm, s32[8,4]{1,0:T(8,128)} %copy.11.slot_hbm, bf16[8,4]{1,0:T(8,128)(2,1)} %copy.12.rw_hbm, bf16[1,2048]{1,0:T(2,128)(2,1)} %reshape.3.sg_ref, bf16[2,2048,1408]{2,1,0:T(8,128)(2,1)} %sgu_hbm.1, ...), custom_call_target="tpu_custom_call" | custom-call | tf_op jit(solution)/shard_map/expert_block/pallas_call | solution.py:316
  39.5 1.4 %copy.15 = bf16[8,2048]{1,0:T(8,128)(2,1)} copy(bf16[8,2048]{1,0:T(8,128)(2,1)} %expert_block.1) | data formatting | bytes 65536

commit v2 on v1

--- a/solution.py
+++ b/solution.py
@@ -99,6 +99,10 @@
     return picked
 
 
+def by_rows(left, right):
+    return lax.dot_general(left, right, (((1,), (1,)), ((), ())), preferred_element_type=jnp.float32)
+
+
 def block_kernel(
     planes,
     tok_hbm,
@@ -141,7 +145,7 @@
     d = lax.axis_index("depth")
     t = lax.axis_index("tok")
     rows, width = tok_hbm.shape
-    choices = ids_hbm.shape[1]
+    choices = ids_hbm.shape[0]
     shared_units = sdn_hbm.shape[0]
     panel = sdn_v.shape[0]
     chunks = st.shape[0]
@@ -180,16 +184,18 @@
 
     for copy in small:
         copy.wait()
-    lane = lax.broadcasted_iota(jnp.int32, (rows, LANES), 1)
+    expert = lax.broadcasted_iota(jnp.int32, (LANES, rows), 0)
     ids = ids_v[...]
     slots = slot_v[...]
     weights = rw_v[...].astype(jnp.float32)
     capacity = max(2, rows * choices // planes)
-    share = jnp.zeros((rows, LANES), jnp.float32)
+    share = jnp.zeros((LANES, rows), jnp.float32)
     for k in range(choices):
-        hit = (ids[:, k : k + 1] == lane) & (slots[:, k : k + 1] < capacity)
-        share = share + jnp.where(hit, weights[:, k : k + 1], 0.0)
-    xb[p, :, width:] = share.astype(jnp.bfloat16)
+        hit = (ids[k : k + 1] == expert) & (slots[k : k + 1] < capacity)
+        share = share + jnp.where(hit, weights[k : k + 1], 0.0)
+    same_row = lax.broadcasted_iota(jnp.int32, (rows, rows), 0) == lax.broadcasted_iota(jnp.int32, (rows, rows), 1)
+    turned = by_rows(same_row.astype(jnp.bfloat16), share.astype(jnp.bfloat16))
+    xb[p, :, width:] = turned.astype(jnp.bfloat16)
     tok_copy.wait()
     pl.semaphore_wait(barrier, planes + 1)
 
@@ -255,20 +261,17 @@
     total = xb.shape[0] * rows
     x = xb[:, :, :width].reshape(total, width)
 
-    def gated(gate_up):
-        gate_part = jnp.dot(x, gate_up[0], preferred_element_type=jnp.float32)
-        up_part = jnp.dot(x, gate_up[1], preferred_element_type=jnp.float32)
-        return jax.nn.silu(gate_part) * up_part
-
-    expert_hidden = gated(egu_v).astype(jnp.bfloat16)
-    shared_hidden = gated(sgu_v)
+    expert_hidden = (jax.nn.silu(by_rows(x, egu_v[0])) * by_rows(x, egu_v[1])).astype(jnp.bfloat16)
+    gate_part = jnp.dot(x, sgu_v[0], preferred_element_type=jnp.float32)
+    up_part = jnp.dot(x, sgu_v[1], preferred_element_type=jnp.float32)
+    shared_hidden = jax.nn.silu(gate_part) * up_part
     unit = start + lax.broadcasted_iota(jnp.int32, shared_hidden.shape, 1)
     shared_hidden = jnp.where(unit >= shard * panel, shared_hidden, 0.0).astype(jnp.bfloat16)
     column = lax.broadcasted_iota(jnp.int32, (total, LANES), 1)
     meta = xb[:, :, width:].reshape(total, LANES).astype(jnp.float32)
     route = jnp.sum(jnp.where(column == p, meta, 0.0), axis=1, keepdims=True)
     gate_rows = jnp.broadcast_to(sg_ref[...].reshape(1, width), (8, width))
-    score = lax.dot_general(x, gate_rows, (((1,), (1,)), ((), ())), preferred_element_type=jnp.float32)
+    score = by_rows(x, gate_rows)
     scale = jax.nn.sigmoid(score[:, :1])
 
     for copy in down_copies:
@@ -320,12 +323,12 @@
         out_specs=vmem,
         scratch_shapes=[
             pltpu.VMEM((blocks, rows, width + LANES), bf16),
-            pltpu.VMEM(expert_ids.shape, jnp.int32),
-            pltpu.VMEM(slot_index.shape, jnp.int32),
-            pltpu.VMEM(route_weight.shape, bf16),
+            pltpu.VMEM(expert_ids.shape[::-1], jnp.int32),
+            pltpu.VMEM(slot_index.shape[::-1], jnp.int32),
+            pltpu.VMEM(route_weight.shape[::-1], bf16),
             pltpu.VMEM((2, width, panel), bf16),
             pltpu.VMEM((panel, width), bf16),
-            pltpu.VMEM(expert_gate_up.shape[1:], bf16),
+            pltpu.VMEM((2, expert_gate_up.shape[3], width), bf16),
             pltpu.VMEM(expert_down.shape[1:], bf16),
             pltpu.VMEM((chunks, 2 * planes * rows, span), f32),
             pltpu.VMEM((chunks, 2 * planes * rows, span), bf16),
@@ -347,7 +350,7 @@
         ],
         compiler_params=pltpu.CompilerParams(collective_id=0, has_side_effects=True),
         name="expert_block",
-    )(tokens, expert_ids, slot_index, route_weight, shared_gate.reshape(1, width), shared_gate_up, shared_down, expert_gate_up, expert_down)
+    )(tokens, expert_ids.T, slot_index.T, route_weight.T, shared_gate, shared_gate_up, shared_down, jnp.swapaxes(expert_gate_up, 2, 3), expert_down)
 
 
 def on_any_device(mesh, tokens, expert_ids, slot_index, route_weight, shared_gate, shared_gate_up, shared_down, expert_gate_up, expert_down):

time: 41.2 us -> 31.5 us (0.76)
  local copies, waits for them, and re-layouts: 11.3 us -> 1.38 us
    unnamed x5 -> x1, local copies, waits for them, and re-layouts: 10 us -> 1.38 us
    reshape x1 -> x0, local copies, waits for them, and re-layouts: 1.29 us -> none  [fused_block(): shared_gate.reshape(1, width)]
where the time goes in v2:
time: 31.5 us; the launch traced here: 31.3 us
  Pallas kernels  29.9 us (95%)
  local copies, waits for them, and re-layouts  1.38 us (4%)
    pallas_call x1, Pallas kernels, fused_block(): pl.pallas_call(functools.partial(block_kernel, planes), out_shape=jax.Sha...  29.9 us
    unnamed x1, local copies, waits for them, and re-layouts  1.38 us

profile of v2, /device:TPU:0, one launch (start us, length us, event | category | flops | bytes accessed | tf_op | source)
XLA Modules:
  0.0 31.3 jit_solution(4391318979340237574)
XLA Ops:
  0.0 29.9 %expert_block.1 = bf16[8,2048]{1,0:T(8,128)(2,1)} custom-call(bf16[8,2048]{1,0:T(8,128)(2,1)} %tok_hbm.1, s32[4,8]{1,0:T(4,128)} %bitcast.5, s32[4,8]{1,0:T(4,128)} %bitcast.6, bf16[4,8]{1,0:T(4,128)(2,1)} %bitcast.7, bf16[2048]{0:T(1024)(128)(2,1)} %sg_ref.1, bf16[2,2048,1408]{2,1,0:T(8,128)(2,1)} %sgu_hbm.1, bf16[1408,2048]{1,0:T(8,128)(2,1)} %sdn_hbm.1, ...), custom_call_target="tpu_custom_call" | custom-call | tf_op jit(solution)/shard_map/expert_block/pallas_call | solution.py:319
  29.9 1.4 %copy.11 = bf16[8,2048]{1,0:T(8,128)(2,1)} copy(bf16[8,2048]{1,0:T(8,128)(2,1)} %expert_block.1) | data formatting | bytes 65536

commit v3 on v2

--- a/solution.py
+++ b/solution.py
@@ -84,7 +84,9 @@
 
 
 LANES = 128
-COLUMN_CHUNKS = 4
+COLUMN_CHUNKS = 8
+T_LAG = 3
+REACH = 2
 MESH = pl.DeviceIdType.MESH
 
 
@@ -170,12 +172,19 @@
         local(slot_hbm, slot_v, 2),
         local(rw_hbm, rw_v, 3),
     ]
+    inner = (p > 0) & (p < planes - 1)
     barrier = pltpu.get_barrier_semaphore()
-    for peer in [{"plane": q} for q in near] + [to_x, to_t]:
+    for peer in [{"plane": q} for q in near[:-1]] + [to_x, to_t]:
         pl.semaphore_signal(barrier, inc=1, device_id=peer, device_id_type=MESH)
+
+    @pl.when(inner)
+    def _():
+        pl.semaphore_signal(barrier, inc=1, device_id={"plane": near[-1]}, device_id_type=MESH)
+
     up_copies = [
         local(egu_hbm.at[0], egu_v, 4),
-        local(sgu_hbm.at[:, :, pl.ds(start, panel)], sgu_v, 5),
+        local(sgu_hbm.at[0, :, pl.ds(start, panel)], sgu_v.at[:, pl.ds(0, panel)], 5),
+        local(sgu_hbm.at[1, :, pl.ds(start, panel)], sgu_v.at[:, pl.ds(panel, panel)], 8),
     ]
     down_copies = [
         local(edn_hbm.at[0], edn_v, 6),
@@ -197,15 +206,15 @@
     turned = by_rows(same_row.astype(jnp.bfloat16), share.astype(jnp.bfloat16))
     xb[p, :, width:] = turned.astype(jnp.bfloat16)
     tok_copy.wait()
-    pl.semaphore_wait(barrier, planes + 1)
+    pl.semaphore_wait(barrier, jnp.where(inner, planes + 1, planes))
 
     def block(rel_t, rel_d, q):
         return xb.at[(rel_t * 2 + rel_d) * planes + q]
 
     pending = []
 
-    def remote(src, dst, send_sem, recv_sem, device):
-        copy = pltpu.make_async_remote_copy(
+    def copy_to(src, dst, send_sem, recv_sem, device):
+        return pltpu.make_async_remote_copy(
             src_ref=src,
             dst_ref=dst,
             send_sem=send_sem,
@@ -213,6 +222,9 @@
             device_id=device,
             device_id_type=MESH,
         )
+
+    def remote(*what):
+        copy = copy_to(*what)
         copy.start()
         pending.append(copy)
 
@@ -226,8 +238,20 @@
             device_id_type=MESH,
         ).wait_recv()
 
-    for q in reversed(near):
-        remote(block(0, 0, p), block(0, 0, p), ag_send.at[0, q], ag_recv.at[0, p], {"plane": q})
+    def own_to(q):
+        return copy_to(block(0, 0, p), block(0, 0, p), ag_send.at[0, q], ag_recv.at[0, p], {"plane": q})
+
+    beside = jnp.where(p == 1, 0, planes - 1)
+    relay = copy_to(block(0, 0, near[-1]), block(0, 0, near[-1]), ag_send.at[4, 0], ag_recv.at[0, near[-1]], {"plane": beside})
+
+    @pl.when(inner)
+    def _():
+        own_to(near[-1]).start()
+
+    for q in reversed(near[:-1]):
+        copy = own_to(q)
+        copy.start()
+        pending.append(copy)
 
     def pass_x(q):
         remote(block(0, 0, q), block(0, 1, q), ag_send.at[1, q], ag_recv.at[1, q], to_x)
@@ -237,6 +261,8 @@
 
     def from_z(q):
         landed(block(0, 0, q), ag_send.at[0, q], ag_recv.at[0, q])
+        if q is near[-1]:
+            pl.when(inner)(relay.start)
         pass_x(q)
         pass_t(0, q)
 
@@ -262,9 +288,8 @@
     x = xb[:, :, :width].reshape(total, width)
 
     expert_hidden = (jax.nn.silu(by_rows(x, egu_v[0])) * by_rows(x, egu_v[1])).astype(jnp.bfloat16)
-    gate_part = jnp.dot(x, sgu_v[0], preferred_element_type=jnp.float32)
-    up_part = jnp.dot(x, sgu_v[1], preferred_element_type=jnp.float32)
-    shared_hidden = jax.nn.silu(gate_part) * up_part
+    both_parts = jnp.dot(x, sgu_v[...], preferred_element_type=jnp.float32)
+    shared_hidden = jax.nn.silu(both_parts[:, :panel]) * both_parts[:, panel:]
     unit = start + lax.broadcasted_iota(jnp.int32, shared_hidden.shape, 1)
     shared_hidden = jnp.where(unit >= shard * panel, shared_hidden, 0.0).astype(jnp.bfloat16)
     column = lax.broadcasted_iota(jnp.int32, (total, LANES), 1)
@@ -276,18 +301,27 @@
 
     for copy in down_copies:
         copy.wait()
-    for c in range(chunks):
+
+    def down(c):
         cols = pl.ds(c * span, span)
         part = route * jnp.dot(expert_hidden, edn_v[:, cols], preferred_element_type=jnp.float32)
         part = part + scale * jnp.dot(shared_hidden, sdn_v[:, cols], preferred_element_type=jnp.float32)
         st[c] = part[half:].astype(jnp.bfloat16)
         remote(st.at[c], rt.at[c], t_send.at[c], t_recv.at[c], to_t)
         keep[c] = part[:half]
-    for c in range(chunks):
+
+    def after_t(c):
         landed(rt.at[c], t_send.at[c], t_recv.at[c])
         sx[c] = (keep[c, quarter:] + rt[c, quarter:].astype(jnp.float32)).astype(jnp.bfloat16)
         remote(sx.at[c], rx.at[c], x_send.at[c], x_recv.at[c], to_x)
         keep[c, :quarter] = keep[c, :quarter] + rt[c, :quarter].astype(jnp.float32)
+
+    for c in range(chunks):
+        down(c)
+        if c >= T_LAG:
+            after_t(c - T_LAG)
+    for c in range(chunks - T_LAG, chunks):
+        after_t(c)
     for c in range(chunks):
         landed(rx.at[c], x_send.at[c], x_recv.at[c])
         value = keep[c, :quarter] + rx[c].astype(jnp.float32)
@@ -304,6 +338,11 @@
         out_ref[:, c * span : (c + 1) * span] = value.astype(jnp.bfloat16)
     for copy in pending:
         copy.wait_send()
+
+    @pl.when(inner)
+    def _():
+        own_to(near[-1]).wait_send()
+        relay.wait_send()
 
 
 def fused_block(planes, tokens, expert_ids, slot_index, route_weight, shared_gate, shared_gate_up, shared_down, expert_gate_up, expert_down):
@@ -326,7 +365,7 @@
             pltpu.VMEM(expert_ids.shape[::-1], jnp.int32),
             pltpu.VMEM(slot_index.shape[::-1], jnp.int32),
             pltpu.VMEM(route_weight.shape[::-1], bf16),
-            pltpu.VMEM((2, width, panel), bf16),
+            pltpu.VMEM((width, 2 * panel), bf16),
             pltpu.VMEM((panel, width), bf16),
             pltpu.VMEM((2, expert_gate_up.shape[3], width), bf16),
             pltpu.VMEM(expert_down.shape[1:], bf16),
@@ -338,8 +377,8 @@
             pltpu.VMEM((chunks, planes, rows, span), f32),
             pltpu.VMEM((chunks, planes, rows, span), bf16),
             pltpu.VMEM((chunks, planes, rows, span), bf16),
-            pltpu.SemaphoreType.DMA((8,)),
-            pltpu.SemaphoreType.DMA((4, planes)),
+            pltpu.SemaphoreType.DMA((9,)),
+            pltpu.SemaphoreType.DMA((5, planes)),
             pltpu.SemaphoreType.DMA((4, planes)),
             pltpu.SemaphoreType.DMA((chunks,)),
             pltpu.SemaphoreType.DMA((chunks,)),
@@ -357,7 +396,8 @@
     args = (tokens, expert_ids, slot_index, route_weight, shared_gate, shared_gate_up, shared_down, expert_gate_up, expert_down)
     planes = mesh.shape["plane"]
     every_expert = expert_ids.shape[1] == planes * expert_gate_up.shape[0] and expert_gate_up.shape[0] == 1
-    pairs = mesh.shape["depth"] == 2 and mesh.shape["tok"] == 2
+    lined = planes == REACH + 2
+    pairs = lined and mesh.shape["depth"] == 2 and mesh.shape["tok"] == 2
     tiled = tokens.shape[1] % (LANES * COLUMN_CHUNKS) == 0 and shared_down.shape[0] % LANES == 0
     if every_expert and pairs and tiled:
         return fused_block(planes, *args)

time: 31.5 us -> 34 us (1.079)
  Pallas kernels: 29.9 us -> 32.4 us
    pallas_call x1, Pallas kernels: 29.9 us -> 32.4 us  [fused_block(): pl.pallas_call(functools.partial(block_kernel, planes), out_shape=jax.Sha...]
where the time goes in v3:
time: 34 us; the launch traced here: 33.8 us
  Pallas kernels  32.4 us (95%)
  local copies, waits for them, and re-layouts  1.38 us (4%)
    pallas_call x1, Pallas kernels, fused_block(): pl.pallas_call(functools.partial(block_kernel, planes), out_shape=jax.Sha...  32.4 us
    unnamed x1, local copies, waits for them, and re-layouts  1.38 us

profile of v3, /device:TPU:0, one launch (start us, length us, event | category | flops | bytes accessed | tf_op | source)
XLA Modules:
  0.0 33.8 jit_solution(6288917062696596287)
XLA Ops:
  0.0 32.4 %expert_block.1 = bf16[8,2048]{1,0:T(8,128)(2,1)} custom-call(bf16[8,2048]{1,0:T(8,128)(2,1)} %tok_hbm.1, s32[4,8]{1,0:T(4,128)} %bitcast.5, s32[4,8]{1,0:T(4,128)} %bitcast.6, bf16[4,8]{1,0:T(4,128)(2,1)} %bitcast.7, bf16[2048]{0:T(1024)(128)(2,1)} %sg_ref.1, bf16[2,2048,1408]{2,1,0:T(8,128)(2,1)} %sgu_hbm.1, bf16[1408,2048]{1,0:T(8,128)(2,1)} %sdn_hbm.1, ...), custom_call_target="tpu_custom_call" | custom-call | tf_op jit(solution)/shard_map/expert_block/pallas_call | solution.py:358
  32.4 1.4 %copy.11 = bf16[8,2048]{1,0:T(8,128)(2,1)} copy(bf16[8,2048]{1,0:T(8,128)(2,1)} %expert_block.1) | data formatting | bytes 65536
